TPU v7x, 32 devices: a whole 2x2x4 slice. The times are simulated.
32 devices in a mesh: batch: 8 (over y, x, core), shard: 4 (over z).
Axes of the slice: x: 2, y: 2, z: 4, core: 2. Of those that a mesh axis runs over, the one named last changes fastest.
Arguments:
- particles: float32 [8192, 1024], P(('batch', 'shard')), may hold values from -48 to 48
- batch_of: int32 [2, 8192], P(None, ('batch', 'shard')), may hold values from 0 to 7, as said below
- mixture_means: float32 [16, 1024], replicated, may hold values from -3 to 3
- log_weights: float32 [16], replicated, may hold values from -2 to 2
Outputs:
- moved: float32 [8192, 1024], P(('batch', 'shard'))
Inputs may be any that keep to these rules, and one draw needn't show every extreme that they name: `batch_of`: in each iteration, the 256 particles of one device hold every batch number equally often, 256 / 8 times each.
All inputs are finite; a program needn't handle non-finite values.
Results may differ from a plain program's by a relative error of at most 0.00011.
Values sent between devices are 32-bit elements; how exact they have to be, the bound alone decides.
A program may use at most 64 MiB of HBM per device.

v0:
```python
import functools

import jax
import jax.numpy as jnp
from jax import lax
from jax.experimental import pallas as pl
from jax.experimental.pallas import tpu as pltpu
from jax.sharding import PartitionSpec as P

variance = 4.0
step_size = 32.0
MESH = pl.DeviceIdType.MESH


def split(a):
    high = a.astype(jnp.bfloat16)
    return high, (a - high.astype(jnp.float32)).astype(jnp.bfloat16)


def dot3(a, b, contract):
    dims = (contract, ((), ()))
    one = functools.partial(lax.dot_general, dimension_numbers=dims, preferred_element_type=jnp.float32)
    return one(a[0], b[0]) + (one(a[0], b[1]) + one(a[1], b[0]))


def step_kernel(
    groups,
    shards,
    rows_ref,
    means_ref,
    logw_ref,
    out_ref,
    pool,
    mine,
    lhs_high,
    lhs_low,
    own_sq,
    acc,
    acc_w,
    acc_k,
    late_high,
    late_low,
    moved,
    own_sem,
    a_send,
    a_recv,
    x_send,
    x_recv,
    c_send,
    c_recv,
    r_send,
    r_recv,
):
    count, width = rows_ref.shape
    chunk = count // groups
    half = count // 2
    members = shards
    pairs = members // 2
    wide = groups // shards
    near = shards // 2
    b = lax.axis_index("batch")
    s = lax.axis_index("shard")
    q, t = b // members, b % members
    x, c = t // 2, t % 2
    g = q * shards + s
    h, l = s // near, s % near

    def piece(index, start=0, rows=chunk):
        return pl.ds(pl.multiple_of(index * chunk + start, 8), rows)

    def group(step, sign):
        far, i, dq = step
        side = 1 - h if far else h
        column = side * near + lax.rem(l + near + sign * i, near)
        return lax.rem(q + wide + sign * dq, wide) * shards + column

    def place(index):
        return (index // shards) * members + t, index % shards

    def mate(j, other):
        return q * members + lax.rem(x + j, pairs) * 2 + (1 - c if other else c), s

    self_step = (0, 0, 0)
    same = [(0, 0, dq) for dq in range(1, wide)]
    close = [(0, i, dq) for i in range(1, near) for dq in range(wide)]
    far = [(1, i, dq) for i in range(near) for dq in range(wide)]
    mixed_order = []
    for n in range(max(len(far), len(close))):
        mixed_order += far[n : n + 1] + close[n : n + 1]
    steps = [self_step] + same + mixed_order
    items = []
    for n, at in enumerate(steps):
        if n >= groups - 2:
            items += [(at, 0, chunk // 2), (at, chunk // 2, chunk // 2)]
        else:
            items.append((at, 0, chunk))

    barrier = pltpu.get_barrier_semaphore()
    targets = [place(group(at, 1)) for at in steps[1:]]
    targets += [mate(j, False) for j in range(1, pairs)] + [mate(0, True)]
    for target in targets:
        pl.semaphore_signal(barrier, inc=1, device_id=target, device_id_type=MESH)
    pl.semaphore_wait(barrier, len(targets))

    own = pltpu.make_async_copy(rows_ref.at[piece(g)], pool.at[t, piece(g)], own_sem.at[0])
    own.start()
    sends = [own]
    for n, (at, start, rows) in enumerate(items[1:], 1):
        to = group(at, 1)
        sends.append(
            pltpu.make_async_remote_copy(
                src_ref=rows_ref.at[piece(to, start, rows)],
                dst_ref=pool.at[t, piece(g, start, rows)],
                send_sem=a_send.at[n],
                recv_sem=a_recv.at[n],
                device_id=place(to),
                device_id_type=MESH,
            )
        )
        sends[-1].start()

    def pass_on(j, n, other):
        at, start, rows = items[n]
        source = piece(group(at, -1), start, rows)
        block = lax.rem(x + pairs - (j if other else 0), pairs) * 2 + c
        sem = (c_send, c_recv) if other else (x_send, x_recv)
        copy = pltpu.make_async_remote_copy(
            src_ref=pool.at[block, source],
            dst_ref=pool.at[block, source],
            send_sem=sem[0].at[j, n],
            recv_sem=sem[1].at[j, n],
            device_id=mate(0, True) if other else mate(j, False),
            device_id_type=MESH,
        )
        copy.start()
        return copy

    across, inside = {}, {}
    for n in range(len(items)):
        if n == 0:
            own.wait()
        else:
            sends[n].wait_recv()
        for j in range(1, pairs):
            across[j, n] = pass_on(j, n, False)
        inside[0, n] = pass_on(0, n, True)
        if n >= 2:
            for j in range(1, pairs):
                across[j, n - 2].wait_recv()
                inside[j, n - 2] = pass_on(j, n - 2, True)

    means = means_ref[...]
    mean_parts = split(means)
    mean_sq = jnp.sum(means * means, axis=1, keepdims=True)
    back_order = far + close + same + [self_step]
    for n, at in enumerate(back_order):
        block = pool[t, piece(group(at, 1))]
        high, low = split(block)
        spot = slice(n * chunk, (n + 1) * chunk)
        mine[spot, :] = block
        lhs_high[spot, :] = high
        lhs_low[spot, :] = low
        own_sq[spot, :] = jnp.sum(block * block, axis=1, keepdims=True)
    lhs_high[count:, :] = mean_parts[0]
    lhs_low[count:, :] = mean_parts[1]

    def process(block, first):
        points = pool[block]
        parts = split(points)
        sq = jnp.sum(points * points, axis=1, keepdims=True)
        sq_row = jnp.transpose(jnp.broadcast_to(sq, (count, 128)))[0:1, :]
        crossed = dot3((lhs_high[...], lhs_low[...]), parts, ((1,), (1,)))
        kernel = jnp.exp(-(own_sq[...] + sq_row - 2.0 * crossed[:count]) * (2.0 / width))
        logits = logw_ref[...] - (sq_row - 2.0 * crossed[count:] + mean_sq) / (2.0 * variance)
        weights = jnp.exp(logits - jnp.max(logits, axis=0, keepdims=True))
        weights = weights / jnp.sum(weights, axis=0, keepdims=True)
        high, low = split(kernel)
        late_high[block] = high[half:]
        late_low[block] = low[half:]
        point = dot3((high[:half], low[:half]), parts, ((1,), (0,)))
        mixed = dot3((high, low), split(weights), ((1,), (1,)))
        total = jnp.sum(kernel, axis=1, keepdims=True)
        if first:
            acc[...] = point
            acc_w[...] = mixed
            acc_k[...] = total
        else:
            acc[...] += point
            acc_w[...] += mixed
            acc_k[...] += total

    process(t, True)

    for n in range(len(items) - 2, len(items)):
        for j in range(1, pairs):
            across[j, n].wait_recv()
            inside[j, n] = pass_on(j, n, True)
    for copy in inside.values():
        copy.wait_recv()

    def rest(i, carry):
        j, e = i // 2, i % 2
        process(lax.rem(x + pairs - j, pairs) * 2 + lax.rem(c + e, 2), False)
        return carry

    lax.fori_loop(1, members, rest, 0)

    size = count * members
    scale = 4.0 / width
    back = []

    def finish(first):
        span = slice(first, first + half)
        pulled = dot3(split(acc_w[span, :]), mean_parts, ((1,), (0,)))
        rows = mine[span, :]
        drift = (pulled - acc[...]) / variance + scale * (rows * acc_k[span, :] - acc[...])
        moved[span, :] = rows + (step_size / size) * drift
        for n in range(first // chunk, (first + half) // chunk):
            spot = slice(n * chunk, (n + 1) * chunk)
            to = group(back_order[n], 1)
            if n == groups - 1:
                copy = pltpu.make_async_copy(moved.at[spot], out_ref.at[piece(g)], own_sem.at[1])
            else:
                copy = pltpu.make_async_remote_copy(
                    src_ref=moved.at[spot],
                    dst_ref=out_ref.at[piece(g)],
                    send_sem=r_send.at[n],
                    recv_sem=r_recv.at[n],
                    device_id=place(to),
                    device_id_type=MESH,
                )
            copy.start()
            back.append(copy)

    finish(0)

    def later(block, carry):
        point = dot3((late_high[block], late_low[block]), split(pool[block]), ((1,), (0,)))
        acc[...] += point
        return carry

    acc[...] = jnp.zeros_like(acc)
    lax.fori_loop(0, members, later, 0)
    finish(half)

    for copy in sends[1:]:
        copy.wait_send()
    for copy in across.values():
        copy.wait_send()
    for copy in inside.values():
        copy.wait_send()
    for copy in back:
        copy.wait()


def step(rows, means, logw, groups, shards):
    count, width = rows.shape
    components = means.shape[0]
    pairs = shards // 2
    dma = pltpu.SemaphoreType.DMA
    return pl.pallas_call(
        functools.partial(step_kernel, groups, shards),
        out_shape=jax.ShapeDtypeStruct((count, width), jnp.float32),
        in_specs=[pl.BlockSpec(memory_space=pltpu.VMEM)] * 3,
        out_specs=pl.BlockSpec(memory_space=pltpu.VMEM),
        scratch_shapes=[
            pltpu.VMEM((shards, count, width), jnp.float32),
            pltpu.VMEM((count, width), jnp.float32),
            pltpu.VMEM((count + components, width), jnp.bfloat16),
            pltpu.VMEM((count + components, width), jnp.bfloat16),
            pltpu.VMEM((count, 1), jnp.float32),
            pltpu.VMEM((count // 2, width), jnp.float32),
            pltpu.VMEM((count, components), jnp.float32),
            pltpu.VMEM((count, 1), jnp.float32),
            pltpu.VMEM((shards, count // 2, count), jnp.bfloat16),
            pltpu.VMEM((shards, count // 2, count), jnp.bfloat16),
            pltpu.VMEM((count, width), jnp.float32),
            dma((2,)),
            dma((groups + 2,)),
            dma((groups + 2,)),
            dma((pairs, groups + 2)),
            dma((pairs, groups + 2)),
            dma((pairs, groups + 2)),
            dma((pairs, groups + 2)),
            dma((groups,)),
            dma((groups,)),
        ],
        compiler_params=pltpu.CompilerParams(
            collective_id=0, has_side_effects=True, vmem_limit_bytes=48 * 1024 * 1024
        ),
    )(rows, means, logw)


def permutation(batch, groups):
    count = batch.shape[0]
    chunk = count // groups
    index = jnp.arange(count, dtype=jnp.int32)
    same = (batch[:, None] == batch[None, :]) & (index[:, None] < index[None, :])
    spot = batch * chunk + jnp.sum(same.astype(jnp.int32), axis=0)
    return (index[:, None] == spot[None, :]).astype(jnp.float32)


def apply(matrix, rows, transposed=False):
    dims = (((0,), (0,)) if transposed else ((1,), (0,)), ((), ()))
    return lax.dot_general(
        matrix, rows, dims, precision=lax.Precision.HIGHEST, preferred_element_type=jnp.float32
    )


def body(particles, batch_of, mixture_means, log_weights):
    groups = lax.axis_size("batch")
    shards = lax.axis_size("shard")
    logw = log_weights[:, None]
    current = particles
    previous = None
    for iteration in range(batch_of.shape[0]):
        order = permutation(batch_of[iteration], groups)
        if previous is None:
            current = apply(order, current)
        else:
            both = lax.dot_general(
                order.astype(jnp.bfloat16),
                previous.astype(jnp.bfloat16),
                (((1,), (1,)), ((), ())),
                preferred_element_type=jnp.float32,
            )
            current = apply(both, current)
        current = step(current, mixture_means, logw, groups, shards)
        previous = order
    return apply(previous, current, transposed=True)


def solution(mesh):
    placed = (P(("batch", "shard"), None), P(None, ("batch", "shard")), P(), P())
    return jax.shard_map(
        body, mesh=mesh, in_specs=placed, out_specs=P(("batch", "shard"), None), check_vma=False
    )
```

profile of v0, /device:TPU:0, one launch (start us, length us, event | category | flops | bytes accessed | tf_op | source)
XLA Modules:
  0.0 129.6 jit_solution(14754163323513596812)
XLA Ops:
  0.0 0.0 copy-start
  0.0 0.8 fusion.9
  0.8 0.1 convert_reduce_fusion.1
  0.9 0.0 copy-start.2
  0.9 0.1 convert_reduce_fusion
  1.0 0.6 copy-done.2
  1.6 0.0 copy-start.3
  1.6 0.7 copy-done.3
  2.3 0.1 copy.7.logw_ref
  2.3 0.2 fusion.4
  2.6 0.0 copy-done
  2.6 0.0 copy-start.1
  2.6 0.7 fusion.rows_ref
  3.3 0.1 copy-done.1
  3.4 61.7 %shard_map.46 = f32[256,1024]{1,0:T(8,128)S(1)} custom-call(f32[256,1024]{1,0:T(8,128)S(1)} %fusion.rows_ref, f32[16,1024]{1,0:T(8,128)S(1)} %copy-done.1, f32[16,1]{1,0:T(8,128)S(1)} %copy.7.logw_ref), custom_call_target="tpu_custom_call" | custom-call | tf_op jit(solution)/shard_map/pallas_call | solution.py:261
  65.1 1.0 fusion.10.rows_ref
  66.2 61.8 %shard_map.47 = f32[256,1024]{1,0:T(8,128)S(1)} custom-call(f32[256,1024]{1,0:T(8,128)S(1)} %fusion.10.rows_ref, f32[16,1024]{1,0:T(8,128)S(1)} %copy-done.1, f32[16,1]{1,0:T(8,128)S(1)} %copy.7.logw_ref), custom_call_target="tpu_custom_call" | custom-call | tf_op jit(solution)/shard_map/pallas_call | solution.py:261
  127.9 1.7 %fusion.3 = f32[256,1024]{1,0:T(8,128)} fusion(f32[256,1024]{1,0:T(8,128)S(1)} %shard_map.47, s32[256]{0:T(256)S(1)} %bitcast.12), kind=kOutput, calls=%fused_computation.10 | convolution fusion | flops 805371904 | bytes 2098176 | tf_op jit(solution)/shard_map/dot_general | solution.py:305
  (1 shorter events, 0.0 us)
Async XLA Ops:
  0.0 2.6 %copy-start = (f32[256,1024]{1,0:T(8,128)S(1)}, f32[256,1024]{1,0:T(8,128)}, u32[]{:S(2)}) copy-start(f32[256,1024]{1,0:T(8,128)} %param.4) | copy-start | bytes 3145732
  0.9 0.7 copy-start.2
  1.6 0.7 copy-start.3
  2.6 0.8 copy-start.1
where the time goes:
time: 132 us; the launch traced here: 130 us
  Pallas kernels  123 us (93%)
  matrix products  3.66 us (3%)
  local copies, waits for them, and re-layouts  2.23 us (2%)
    pallas_call x2, Pallas kernels, step(): pl.pallas_call(functools.partial(step_kernel, groups, shards), out_shape=...  123 us
    dot_general x3, matrix products, apply(): lax.dot_general(matrix, rows, dims, precision=lax.Precision.HIGHEST, pref...  3.41 us

commit v1 on v0

v1 whole, which is shorter than its diff:
```python
import functools

import jax
import jax.numpy as jnp
from jax import lax
from jax.experimental import pallas as pl
from jax.experimental.pallas import tpu as pltpu
from jax.sharding import PartitionSpec as P

variance = 4.0
step_size = 32.0
PARTS = 2
MESH = pl.DeviceIdType.MESH
f32, bf16 = jnp.float32, jnp.bfloat16


def split(a):
    high = a.astype(bf16)
    return high, (a - high.astype(f32)).astype(bf16)


def dot(a, b, contract=((1,), (0,))):
    return lax.dot_general(a, b, (contract, ((), ())), preferred_element_type=f32)


def dot3(a, b, contract=((1,), (0,))):
    return dot(a[0], b[0], contract) + (dot(a[0], b[1], contract) + dot(a[1], b[0], contract))


def permute(matrix, rows):
    high, rest = rows.astype(bf16), None
    rest = rows - high.astype(f32)
    middle, low = split(rest)
    return dot(matrix, high) + (dot(matrix, middle) + dot(matrix, low))


def orders(batch, chunk):
    count = batch.shape[1]
    down = lax.broadcasted_iota(jnp.int32, (count, count), 0)
    along = lax.broadcasted_iota(jnp.int32, (count, count), 1)
    column = jnp.sum(jnp.where(down == along, batch, 0), axis=1, keepdims=True)
    same = column == batch
    rank_row = jnp.sum(jnp.where(same & (down < along), 1, 0), axis=0, keepdims=True)
    rank_column = jnp.sum(jnp.where(same & (along < down), 1, 0), axis=1, keepdims=True)
    there = jnp.where(down == batch * chunk + rank_row, 1.0, 0.0).astype(bf16)
    back = jnp.where(along == column * chunk + rank_column, 1.0, 0.0).astype(bf16)
    return there, back


def kernel(
    groups,
    shards,
    iters,
    x_ref,
    batch_ref,
    means_ref,
    logw_ref,
    out_ref,
    start,
    sent,
    pool,
    moved,
    home,
    final,
    x_high,
    x_low,
    k_high,
    k_low,
    lhs_high,
    lhs_low,
    own_sq,
    acc_w,
    acc_k,
    local_sem,
    a_send,
    a_recv,
    x_send,
    x_recv,
    c_send,
    c_recv,
    r_send,
    r_recv,
):
    count, width = x_ref.shape
    chunk = count // groups
    members = shards
    pairs = members // 2
    wide = groups // shards
    near = shards // 2
    parts = PARTS
    cols = width // parts
    b = lax.axis_index("batch")
    s = lax.axis_index("shard")
    q, t = b // members, b % members
    x, c = t // 2, t % 2
    g = q * shards + s
    side, l = s // near, s % near
    e = (1 - side) * (near - 1 - l) + side * l

    def shard_at(side_at, e_at):
        return (1 - side_at) * (near - 1 - e_at) + side_at * (near + e_at)

    def place(q_at, s_at):
        return q_at * members + t, s_at

    def mate(j, other):
        return q * members + lax.rem(x + j, pairs) * 2 + (1 - c if other else c), s

    def rows_of(index, size=chunk):
        return pl.ds(pl.multiple_of(index * size, 8), size)

    def part(p):
        return slice(p * cols, (p + 1) * cols)

    def slot(far, a, dq):
        return (far * near + a) * wide + dq

    slots = [(far, a, dq) for far in range(2) for a in range(near) for dq in range(wide)]

    def source(k):
        far, a, dq = slots[k]
        q_at = lax.rem(q + wide - dq, wide)
        if far:
            return q_at, shard_at(1 - side, a)
        return q_at, shard_at(side, lax.rem(e + a, near))

    def remote(src, dst, send, recv, device):
        return pltpu.make_async_remote_copy(
            src_ref=src, dst_ref=dst, send_sem=send, recv_sem=recv, device_id=device, device_id_type=MESH
        )

    load = pltpu.make_async_copy(x_ref, start, local_sem.at[0])
    load.start()
    barrier = pltpu.get_barrier_semaphore()
    targets = [place(*source(k)) for k in range(1, groups)]
    targets += [mate(j, False) for j in range(1, pairs)] + [mate(0, True)]
    for target in targets:
        pl.semaphore_signal(barrier, inc=1, device_id=target, device_id_type=MESH)

    logw = logw_ref[...]
    means = means_ref[...]
    mean_parts = split(means)
    mean_sq = jnp.sum(means * means, axis=1, keepdims=True)
    lhs_high[count:, :] = mean_parts[0]
    lhs_low[count:, :] = mean_parts[1]

    there, back = orders(batch_ref[0:1, :], chunk)
    load.wait()
    for p in range(parts):
        sent[0, :, part(p)] = permute(there, start[:, part(p)])
    pl.semaphore_wait(barrier, len(targets))

    def arrival(it, k, p):
        spot = pool.at[it, t, rows_of(k), part(p)]
        return remote(spot, spot, a_send.at[k, p], a_recv.at[k, p], place(*source(k)))

    def send_in(it, k_send, k_recv, q_at, s_at, p):
        to = q_at * shards + s_at
        copy = remote(
            sent.at[it, rows_of(to), part(p)],
            pool.at[it, t, rows_of(k_recv), part(p)],
            a_send.at[k_send, p],
            a_recv.at[k_recv, p],
            place(q_at, s_at),
        )
        copy.start()
        return copy

    def send_near(it, p):
        copies = []
        for r in range(near):
            for dq in range(wide):
                k = slot(0, r, dq)
                if k == 0:
                    pool[it, t, 0:chunk, part(p)] = sent[it, rows_of(g), part(p)]
                else:
                    s_at = shard_at(side, lax.rem(e + near - r, near))
                    copies.append(send_in(it, k, k, lax.rem(q + dq, wide), s_at, p))
        return copies

    def send_far(it, e_at, p):
        copies = []
        for dq in range(wide):
            k_recv = (near + e) * wide + dq
            copies.append(
                send_in(it, slot(1, e_at, dq), k_recv, lax.rem(q + dq, wide), shard_at(1 - side, e_at), p)
            )
        return copies

    def pass_on(it, j, k, p, other):
        block = lax.rem(x + pairs - (j if other else 0), pairs) * 2 + c
        spot = pool.at[it, block, rows_of(k), part(p)]
        sem = (c_send, c_recv) if other else (x_send, x_recv)
        copy = remote(
            spot, spot, sem[0].at[it, j, k, p], sem[1].at[it, j, k, p], mate(0, True) if other else mate(j, False)
        )
        copy.start()
        return copy

    def gather(it):
        half = groups // 2
        pieces = [(k, p) for p in range(parts) for k in range(half)]
        pieces += [(k, p) for p in range(parts) for k in range(half, groups)]
        lag = 2
        across, inside = {}, {}
        for n in range(len(pieces) + lag):
            if n < len(pieces):
                k, p = pieces[n]
                if k:
                    arrival(it, k, p).wait_recv()
                for j in range(1, pairs):
                    across[j, n] = pass_on(it, j, k, p, False)
                inside[0, n] = pass_on(it, 0, k, p, True)
            if n >= lag:
                for j in range(1, pairs):
                    across[j, n - lag].wait_recv()
                    inside[j, n - lag] = pass_on(it, j, *pieces[n - lag], True)
        for copy in inside.values():
            copy.wait_recv()
        return list(across.values()) + list(inside.values())

    def grams(it):
        own = pool[it, t]
        high, low = split(own)
        lhs_high[0:count, :] = high
        lhs_low[0:count, :] = low
        own_sq[...] = jnp.sum(own * own, axis=1, keepdims=True)
        acc_w[...] = jnp.zeros_like(acc_w)
        acc_k[...] = jnp.zeros_like(acc_k)

        def block(m, carry):
            points = pool[it, m]
            both = split(points)
            x_high[m] = both[0]
            x_low[m] = both[1]
            sq = jnp.sum(points * points, axis=1, keepdims=True)
            sq_row = jnp.transpose(jnp.broadcast_to(sq, (count, 128)))[0:1, :]
            crossed = dot3((lhs_high[...], lhs_low[...]), both, ((1,), (1,)))
            values = jnp.exp(-(own_sq[...] + sq_row - 2.0 * crossed[:count]) * (2.0 / width))
            logits = logw - (sq_row - 2.0 * crossed[count:] + mean_sq) / (2.0 * variance)
            weights = jnp.exp(logits - jnp.max(logits, axis=0, keepdims=True))
            weights = weights / jnp.sum(weights, axis=0, keepdims=True)
            pair = split(values)
            k_high[m] = pair[0]
            k_low[m] = pair[1]
            acc_w[...] += dot3(pair, split(weights), ((1,), (1,)))
            acc_k[...] += jnp.sum(values, axis=1, keepdims=True)
            return carry

        lax.fori_loop(0, members, block, 0)

    def send_back(it, p):
        total = None
        for m in range(members):
            pair = (k_high[m], k_low[m])
            one = dot3(pair, (x_high[m, :, part(p)], x_low[m, :, part(p)]))
            total = one if total is None else total + one
        pulled = dot3(split(acc_w[...]), (mean_parts[0][:, part(p)], mean_parts[1][:, part(p)]))
        rows = pool[it, t, :, part(p)]
        drift = (pulled - total) / variance + (4.0 / width) * (rows * acc_k[...] - total)
        moved[it, :, part(p)] = rows + (step_size / (count * members)) * drift
        copies = []
        for k in list(range(groups // 2, groups)) + list(range(1, groups // 2)):
            far, a, dq = slots[k]
            k_recv = (near + e) * wide + dq if far else k
            copy = remote(
                moved.at[it, rows_of(k), part(p)],
                home.at[it, rows_of(g), part(p)],
                r_send.at[k, p],
                r_recv.at[k_recv, p],
                place(*source(k)),
            )
            copy.start()
            copies.append(copy)
        home[it, rows_of(g), part(p)] = moved[it, 0:chunk, part(p)]
        return copies

    def wait_home(it, p):
        for k in range(1, groups):
            far, a, dq = slots[k]
            if far:
                q_at, s_at = lax.rem(q + dq, wide), shard_at(1 - side, a)
            else:
                q_at, s_at = lax.rem(q + dq, wide), shard_at(side, lax.rem(e + near - a, near))
            spot = home.at[it, rows_of(q_at * shards + s_at), part(p)]
            remote(spot, spot, r_send.at[k, p], r_recv.at[k, p], place(q_at, s_at)).wait_recv()

    sends = []
    for p in range(parts):
        sends += send_near(0, p)
    for e_at in range(near):
        for p in range(parts):
            sends += send_far(0, e_at, p)
    for it in range(iters):
        sends += gather(it)
        grams(it)
        returns = []
        for p in range(parts):
            returns += send_back(it, p)
        for copy in sends:
            copy.wait_send()
        sends = []
        last = it == iters - 1
        if not last:
            next_there, next_back = orders(batch_ref[it + 1 : it + 2, :], chunk)
            turn = dot(next_there, back).astype(bf16)
            back = next_back
        stores = []
        for p in range(parts):
            wait_home(it, p)
            block = home[it, :, part(p)]
            if last:
                final[:, part(p)] = permute(back, block)
                store = pltpu.make_async_copy(
                    final.at[:, part(p)], out_ref.at[:, part(p)], local_sem.at[1 + p]
                )
                store.start()
                stores.append(store)
            else:
                sent[it + 1, :, part(p)] = permute(turn, block)
                sends += send_near(it + 1, p)
                sends += send_far(it + 1, 0, p)
        if not last:
            for e_at in range(1, near):
                for p in range(parts):
                    sends += send_far(it + 1, e_at, p)
        for copy in returns:
            copy.wait_send()
        for store in stores:
            store.wait()


def body(particles, batch_of, mixture_means, log_weights):
    groups = lax.axis_size("batch")
    shards = lax.axis_size("shard")
    iters = batch_of.shape[0]
    count, width = particles.shape
    components = mixture_means.shape[0]
    pairs = shards // 2
    dma = pltpu.SemaphoreType.DMA
    vmem = pl.BlockSpec(memory_space=pltpu.VMEM)
    return pl.pallas_call(
        functools.partial(kernel, groups, shards, iters),
        out_shape=jax.ShapeDtypeStruct((count, width), f32),
        in_specs=[pl.BlockSpec(memory_space=pl.ANY), vmem, vmem, vmem],
        out_specs=pl.BlockSpec(memory_space=pl.ANY),
        scratch_shapes=[
            pltpu.VMEM((count, width), f32),
            pltpu.VMEM((iters, count, width), f32),
            pltpu.VMEM((iters, shards, count, width), f32),
            pltpu.VMEM((iters, count, width), f32),
            pltpu.VMEM((iters, count, width), f32),
            pltpu.VMEM((count, width), f32),
            pltpu.VMEM((shards, count, width), bf16),
            pltpu.VMEM((shards, count, width), bf16),
            pltpu.VMEM((shards, count, count), bf16),
            pltpu.VMEM((shards, count, count), bf16),
            pltpu.VMEM((count + components, width), bf16),
            pltpu.VMEM((count + components, width), bf16),
            pltpu.VMEM((count, 1), f32),
            pltpu.VMEM((count, components), f32),
            pltpu.VMEM((count, 1), f32),
            dma((1 + PARTS,)),
            dma((groups, PARTS)),
            dma((groups, PARTS)),
            dma((iters, pairs, groups, PARTS)),
            dma((iters, pairs, groups, PARTS)),
            dma((iters, pairs, groups, PARTS)),
            dma((iters, pairs, groups, PARTS)),
            dma((groups, PARTS)),
            dma((groups, PARTS)),
        ],
        compiler_params=pltpu.CompilerParams(
            collective_id=0, has_side_effects=True, vmem_limit_bytes=58 * 1024 * 1024
        ),
    )(particles, batch_of, mixture_means, log_weights[:, None])


def solution(mesh):
    placed = (P(("batch", "shard"), None), P(None, ("batch", "shard")), P(), P())
    return jax.shard_map(
        body, mesh=mesh, in_specs=placed, out_specs=P(("batch", "shard"), None), check_vma=False
    )
```

time: 132 us -> 133 us (level); the launches traced: 130 us -> 133 us
  Pallas kernels: 123 us -> 129 us
  matrix products: 3.66 us -> 0 us
  local copies, waits for them, and re-layouts: 2.23 us -> 3.64 us
    pallas_call x2 -> x1, Pallas kernels: 123 us -> 129 us  [body(): pl.pallas_call(functools.partial(kernel, groups, shards, iters), out_shap...]
    dot_general x4 -> x0, matrix products: 3.66 us -> none  [the longest x3 3.41 us: apply(): lax.dot_general(matrix, rows, dims, precision=lax.Precision.HIGHEST, pref...]
    unnamed x8 -> x3, local copies, waits for them, and re-layouts: 1.36 us -> 2.96 us
where the time goes in v1:
time: 133 us
  Pallas kernels  129 us (97%)
  local copies, waits for them, and re-layouts  3.64 us (3%)
    pallas_call x1, Pallas kernels, body(): pl.pallas_call(functools.partial(kernel, groups, shards, iters), out_shap...  129 us
    unnamed x3, local copies, waits for them, and re-layouts  2.96 us

profile of v1, /device:TPU:0, one launch (start us, length us, event | category | flops | bytes accessed | tf_op | source)
XLA Modules:
  0.0 132.9 jit_solution(1410230363509190080)
XLA Ops:
  0.0 0.0 copy-start
  0.0 0.7 copy-done
  0.7 0.7 copy.5.logw_ref
  1.3 129.3 %shard_map.46 = f32[256,1024]{1,0:T(8,128)} custom-call(f32[256,1024]{1,0:T(8,128)} %x_ref.1, s32[2,256]{1,0:T(2,128)} %batch_ref.1, f32[16,1024]{1,0:T(8,128)} %means_ref.1, f32[16,1]{1,0:T(8,128)} %copy.5.logw_ref), custom_call_target="tpu_custom_call" | custom-call | tf_op jit(solution)/shard_map/pallas_call | solution.py:342
  130.6 2.3 %copy.7 = f32[256,1024]{1,0:T(8,128)} copy(f32[256,1024]{1,0:T(8,128)} %shard_map.46) | data formatting | bytes 2097152
Async XLA Ops:
  0.0 0.7 copy-start

commit v2 on v1

--- a/solution.py
+++ b/solution.py
@@ -10,6 +10,7 @@
 variance = 4.0
 step_size = 32.0
 PARTS = 2
+LAG = 6
 MESH = pl.DeviceIdType.MESH
 f32, bf16 = jnp.float32, jnp.bfloat16
 
@@ -52,16 +53,18 @@
     shards,
     iters,
     x_ref,
+    batch_hbm,
+    means_hbm,
+    logw_hbm,
+    final,
     batch_ref,
     means_ref,
     logw_ref,
-    out_ref,
     start,
     sent,
     pool,
     moved,
     home,
-    final,
     x_high,
     x_low,
     k_high,
@@ -119,35 +122,42 @@
 
     def source(k):
         far, a, dq = slots[k]
-        q_at = lax.rem(q + wide - dq, wide)
         if far:
-            return q_at, shard_at(1 - side, a)
-        return q_at, shard_at(side, lax.rem(e + a, near))
+            return lax.rem(q + wide - dq, wide), shard_at(1 - side, a)
+        return lax.rem(q + wide - dq, wide), shard_at(side, lax.rem(e + a, near))
 
     def remote(src, dst, send, recv, device):
         return pltpu.make_async_remote_copy(
             src_ref=src, dst_ref=dst, send_sem=send, recv_sem=recv, device_id=device, device_id_type=MESH
         )
 
-    load = pltpu.make_async_copy(x_ref, start, local_sem.at[0])
-    load.start()
+    pairs_of = ((x_ref, start), (batch_hbm, batch_ref), (means_hbm, means_ref), (logw_hbm, logw_ref))
+    loads = [pltpu.make_async_copy(src, dst, local_sem.at[n]) for n, (src, dst) in enumerate(pairs_of)]
+    for load in loads:
+        load.start()
     barrier = pltpu.get_barrier_semaphore()
     targets = [place(*source(k)) for k in range(1, groups)]
     targets += [mate(j, False) for j in range(1, pairs)] + [mate(0, True)]
     for target in targets:
         pl.semaphore_signal(barrier, inc=1, device_id=target, device_id_type=MESH)
 
-    logw = logw_ref[...]
+    loads[1].wait()
+    there, back = orders(batch_ref[0:1, :], chunk)
+    loads[0].wait()
+    for p in range(parts):
+        sent[0, :, part(p)] = permute(there, start[:, part(p)])
+    loads[2].wait()
+    loads[3].wait()
     means = means_ref[...]
+    components = means.shape[0]
+    down = lax.broadcasted_iota(jnp.int32, (components, components), 0)
+    along = lax.broadcasted_iota(jnp.int32, (components, components), 1)
+    logw = jnp.sum(jnp.where(down == along, logw_ref[...], 0.0), axis=1, keepdims=True)
     mean_parts = split(means)
     mean_sq = jnp.sum(means * means, axis=1, keepdims=True)
     lhs_high[count:, :] = mean_parts[0]
     lhs_low[count:, :] = mean_parts[1]
 
-    there, back = orders(batch_ref[0:1, :], chunk)
-    load.wait()
-    for p in range(parts):
-        sent[0, :, part(p)] = permute(there, start[:, part(p)])
     pl.semaphore_wait(barrier, len(targets))
 
     def arrival(it, k, p):
@@ -201,25 +211,25 @@
         half = groups // 2
         pieces = [(k, p) for p in range(parts) for k in range(half)]
         pieces += [(k, p) for p in range(parts) for k in range(half, groups)]
-        lag = 2
+        if it == 0:
+            pieces = [(0, p) for p in range(parts)] + [(k, p) for p in range(parts) for k in range(1, half)]
+            pieces += [(slot(1, a, dq), p) for a in range(near) for p in range(parts) for dq in range(wide)]
         across, inside = {}, {}
-        for n in range(len(pieces) + lag):
-            if n < len(pieces):
-                k, p = pieces[n]
-                if k:
-                    arrival(it, k, p).wait_recv()
-                for j in range(1, pairs):
-                    across[j, n] = pass_on(it, j, k, p, False)
-                inside[0, n] = pass_on(it, 0, k, p, True)
-            if n >= lag:
-                for j in range(1, pairs):
-                    across[j, n - lag].wait_recv()
-                    inside[j, n - lag] = pass_on(it, j, *pieces[n - lag], True)
-        for copy in inside.values():
-            copy.wait_recv()
-        return list(across.values()) + list(inside.values())
-
-    def grams(it):
+
+        def pass_inside(n):
+            for j in range(1, pairs):
+                across[j, n].wait_recv()
+                inside[j, n] = pass_on(it, j, *pieces[n], True)
+
+        for n, (k, p) in enumerate(pieces):
+            if k:
+                arrival(it, k, p).wait_recv()
+            for j in range(1, pairs):
+                across[j, n] = pass_on(it, j, k, p, False)
+            inside[0, n] = pass_on(it, 0, k, p, True)
+            if n >= LAG:
+                pass_inside(n - LAG)
+
         own = pool[it, t]
         high, low = split(own)
         lhs_high[0:count, :] = high
@@ -228,7 +238,7 @@
         acc_w[...] = jnp.zeros_like(acc_w)
         acc_k[...] = jnp.zeros_like(acc_k)
 
-        def block(m, carry):
+        def block(m):
             points = pool[it, m]
             both = split(points)
             x_high[m] = both[0]
@@ -245,9 +255,26 @@
             k_low[m] = pair[1]
             acc_w[...] += dot3(pair, split(weights), ((1,), (1,)))
             acc_k[...] += jnp.sum(values, axis=1, keepdims=True)
-            return carry
-
-        lax.fori_loop(0, members, block, 0)
+
+        def blocks(core):
+            def one(j, carry):
+                block(lax.rem(x + pairs - j, pairs) * 2 + core)
+                return carry
+
+            lax.fori_loop(1, pairs, one, 0)
+
+        block(t)
+        for n in range(len(pieces)):
+            inside[0, n].wait_recv()
+        block(x * 2 + 1 - c)
+        for n in range(len(pieces) - LAG, len(pieces)):
+            pass_inside(n)
+        blocks(c)
+        for (j, n), copy in inside.items():
+            if j:
+                copy.wait_recv()
+        blocks(1 - c)
+        return list(across.values()) + list(inside.values())
 
     def send_back(it, p):
         total = None
@@ -260,7 +287,8 @@
         drift = (pulled - total) / variance + (4.0 / width) * (rows * acc_k[...] - total)
         moved[it, :, part(p)] = rows + (step_size / (count * members)) * drift
         copies = []
-        for k in list(range(groups // 2, groups)) + list(range(1, groups // 2)):
+        fars, nears = list(range(groups // 2, groups)), list(range(1, groups // 2))
+        for k in fars + nears:
             far, a, dq = slots[k]
             k_recv = (near + e) * wide + dq if far else k
             copy = remote(
@@ -293,7 +321,6 @@
             sends += send_far(0, e_at, p)
     for it in range(iters):
         sends += gather(it)
-        grams(it)
         returns = []
         for p in range(parts):
             returns += send_back(it, p)
@@ -305,17 +332,11 @@
             next_there, next_back = orders(batch_ref[it + 1 : it + 2, :], chunk)
             turn = dot(next_there, back).astype(bf16)
             back = next_back
-        stores = []
         for p in range(parts):
             wait_home(it, p)
             block = home[it, :, part(p)]
             if last:
                 final[:, part(p)] = permute(back, block)
-                store = pltpu.make_async_copy(
-                    final.at[:, part(p)], out_ref.at[:, part(p)], local_sem.at[1 + p]
-                )
-                store.start()
-                stores.append(store)
             else:
                 sent[it + 1, :, part(p)] = permute(turn, block)
                 sends += send_near(it + 1, p)
@@ -326,8 +347,6 @@
                     sends += send_far(it + 1, e_at, p)
         for copy in returns:
             copy.wait_send()
-        for store in stores:
-            store.wait()
 
 
 def body(particles, batch_of, mixture_means, log_weights):
@@ -342,15 +361,17 @@
     return pl.pallas_call(
         functools.partial(kernel, groups, shards, iters),
         out_shape=jax.ShapeDtypeStruct((count, width), f32),
-        in_specs=[pl.BlockSpec(memory_space=pl.ANY), vmem, vmem, vmem],
-        out_specs=pl.BlockSpec(memory_space=pl.ANY),
+        in_specs=[pl.BlockSpec(memory_space=pl.ANY)] * 4,
+        out_specs=pl.BlockSpec(memory_space=pltpu.VMEM),
         scratch_shapes=[
+            pltpu.VMEM(batch_of.shape, jnp.int32),
+            pltpu.VMEM(mixture_means.shape, f32),
+            pltpu.VMEM((1, components), f32),
             pltpu.VMEM((count, width), f32),
             pltpu.VMEM((iters, count, width), f32),
             pltpu.VMEM((iters, shards, count, width), f32),
             pltpu.VMEM((iters, count, width), f32),
             pltpu.VMEM((iters, count, width), f32),
-            pltpu.VMEM((count, width), f32),
             pltpu.VMEM((shards, count, width), bf16),
             pltpu.VMEM((shards, count, width), bf16),
             pltpu.VMEM((shards, count, count), bf16),
@@ -360,7 +381,7 @@
             pltpu.VMEM((count, 1), f32),
             pltpu.VMEM((count, components), f32),
             pltpu.VMEM((count, 1), f32),
-            dma((1 + PARTS,)),
+            dma((4,)),
             dma((groups, PARTS)),
             dma((groups, PARTS)),
             dma((iters, pairs, groups, PARTS)),
@@ -373,7 +394,7 @@
         compiler_params=pltpu.CompilerParams(
             collective_id=0, has_side_effects=True, vmem_limit_bytes=58 * 1024 * 1024
         ),
-    )(particles, batch_of, mixture_means, log_weights[:, None])
+    )(particles, batch_of, mixture_means, log_weights[None, :])
 
 
 def solution(mesh):

time: 133 us -> 122 us (0.917)
  Pallas kernels: 129 us -> 120 us
  local copies, waits for them, and re-layouts: 3.64 us -> 2.31 us
    pallas_call x1, Pallas kernels: 129 us -> 120 us  [body(): pl.pallas_call(functools.partial(kernel, groups, shards, iters), out_shap...]
    unnamed x3 -> x1, local copies, waits for them, and re-layouts: 2.96 us -> 2.31 us
where the time goes in v2:
time: 122 us
  Pallas kernels  120 us (98%)
  local copies, waits for them, and re-layouts  2.31 us (2%)
    pallas_call x1, Pallas kernels, body(): pl.pallas_call(functools.partial(kernel, groups, shards, iters), out_shap...  120 us

profile of v2, /device:TPU:0, one launch (start us, length us, event | category | flops | bytes accessed | tf_op | source)
XLA Modules:
  0.0 122.0 jit_solution(315054994373307046)
XLA Ops:
  0.0 119.7 %shard_map.46 = f32[256,1024]{1,0:T(8,128)} custom-call(f32[256,1024]{1,0:T(8,128)} %x_ref.1, s32[2,256]{1,0:T(2,128)} %batch_hbm.1, f32[16,1024]{1,0:T(8,128)} %means_hbm.1, f32[1,16]{1,0:T(1,128)} %bitcast.1), custom_call_target="tpu_custom_call" | custom-call | tf_op jit(solution)/shard_map/pallas_call | solution.py:361
  119.7 2.3 %copy.6 = f32[256,1024]{1,0:T(8,128)} copy(f32[256,1024]{1,0:T(8,128)} %shard_map.46) | data formatting | bytes 2097152
